TPU v7x, 32 devices: a whole 2x2x4 slice. The times are simulated.
32 devices in a mesh: mod: 4 (over y, x), seq: 8 (over z, core).
Axes of the slice: x: 2, y: 2, z: 4, core: 2. Of those that a mesh axis runs over, the one named last changes fastest.
Arguments:
- tokens: bfloat16 [2048, 4096], P(('mod', 'seq')), may hold values from -6 to 6
- norm_gain: float32 [3, 4096], replicated, may hold values from 0.2 to 2.6
- qkv_weight: bfloat16 [3, 4096, 12288], P(None, None, 'seq'), may hold values from -0.45 to 0.45
- out_weight: bfloat16 [3, 4096, 4096], P(None, 'seq'), may hold values from -0.375 to 0.375
- modality: int32 [16], replicated, may hold values from 0 to 2
- doc_lengths: int32 [4], replicated, may hold values from 1 to 1024, 2048 in all
Outputs:
- mixed: bfloat16 [2048, 4096], P(('mod', 'seq'))
Inputs may be any that keep to these rules, and one draw needn't show every extreme that they name: `doc_lengths`: the lengths sum to 2048; documents follow one another from position 0 in the given order.
All inputs are finite; a program needn't handle non-finite values.
Results may differ from a plain program's by a relative error of at most 0.015.
Values may be sent and summed in bfloat16 or wider, within the bound.
A program may use at most 128 MiB of HBM per device.

v0:
```python
import math
import jax
import jax.numpy as jnp
from jax import lax
from jax.sharding import PartitionSpec as P

HDIM = 128
BLOCK = 128


def modes_of_rows(first_row, row_count, modality):
    block_ids = (first_row + jnp.arange(row_count, dtype=jnp.int32)) // BLOCK
    block_table = jnp.arange(modality.shape[0], dtype=jnp.int32)
    picked = jnp.where(block_ids[:, None] == block_table[None, :], modality[None, :], 0)
    return jnp.sum(picked, axis=1)


def documents(positions, doc_lengths):
    doc_ends = jnp.cumsum(doc_lengths)
    return jnp.sum((positions[:, None] >= doc_ends[None, :]).astype(jnp.int32), axis=1)


def body(tokens, norm_gain, qkv_weight, out_weight, modality, doc_lengths):
    row_count = tokens.shape[0]
    seq_count = lax.axis_size("seq")
    mod_count = lax.axis_size("mod")
    group_rows = row_count * seq_count
    mod_index = lax.axis_index("mod")
    own_first = (mod_index * seq_count + lax.axis_index("seq")) * row_count
    row_modes = modes_of_rows(own_first, row_count, modality)
    choose = (
        row_modes[:, None, None] == jnp.arange(norm_gain.shape[0], dtype=jnp.int32)[None, :, None]
    )
    gain_rows = jnp.sum(jnp.where(choose, norm_gain[None, :, :], 0.0), axis=1)
    values = tokens.astype(jnp.float32)
    mean_square = jnp.mean(values * values, axis=1, keepdims=True)
    normed = (values * lax.rsqrt(mean_square + 1e-05) * gain_rows).astype(jnp.bfloat16)
    gathered = lax.all_gather(normed, "seq", axis=0, tiled=True)
    group_first = mod_index * group_rows
    block_count = group_rows // BLOCK
    block_modes = lax.dynamic_slice_in_dim(modality, group_first // BLOCK, block_count)
    heads_here = qkv_weight.shape[2] // (3 * HDIM)

    def project(block_pair):
        row_block, block_mode = block_pair
        weight = lax.dynamic_index_in_dim(qkv_weight, block_mode, 0, keepdims=False)
        return jnp.dot(row_block, weight, preferred_element_type=jnp.float32).astype(jnp.bfloat16)

    projected = lax.map(
        project, (gathered.reshape(block_count, BLOCK, gathered.shape[1]), block_modes)
    )
    projected = projected.reshape(group_rows, heads_here, 3, HDIM)
    queries = projected[:, :, 0, :]
    keys_here = projected[:, :, 1, :]
    values_here = projected[:, :, 2, :]
    quarter = group_rows // mod_count
    local_rows = jnp.arange(group_rows, dtype=jnp.int32)
    query_pos = group_first + local_rows
    query_docs = documents(query_pos, doc_lengths)
    block_size = min(512, quarter)
    block_total = group_rows // block_size
    score_scale = 1.0 / math.sqrt(HDIM)
    query_blocks = queries.reshape(block_total, block_size, heads_here, HDIM)
    pos_blocks = query_pos.reshape(block_total, block_size)
    doc_blocks = query_docs.reshape(block_total, block_size)
    start_state = (
        jnp.full((block_total, heads_here, block_size), -1e30, jnp.float32),
        jnp.zeros((block_total, heads_here, block_size), jnp.float32),
        jnp.zeros((block_total, block_size, heads_here, HDIM), jnp.float32),
    )
    key_start = jnp.int32(0)
    piece_keys = lax.all_gather(keys_here, "mod", axis=0, tiled=True)
    piece_values = lax.all_gather(values_here, "mod", axis=0, tiled=True)
    key_count = piece_keys.shape[0]
    key_pos = jnp.arange(key_count, dtype=jnp.int32)
    key_docs = documents(key_pos, doc_lengths)

    def one_block(block_state):
        row_max, totals, summed_rows, query_block, block_pos, block_docs = block_state

        def attend(unused):
            scores = (
                jnp.einsum(
                    "qhc,khc->hqk", query_block, piece_keys, preferred_element_type=jnp.float32
                )
                * score_scale
            )
            allowed = (
                (key_pos[None, :] <= block_pos[:, None])
                & (key_docs[None, :] == block_docs[:, None])
            )[None, :, :]
            new_max = jnp.maximum(row_max, jnp.max(jnp.where(allowed, scores, -1e30), axis=2))
            weights = jnp.where(allowed, jnp.exp(scores - new_max[:, :, None]), 0.0)
            rescale = jnp.exp(row_max - new_max)
            new_totals = totals * rescale + jnp.sum(weights, axis=2)
            added_rows = jnp.einsum(
                "hqk,khc->qhc",
                weights.astype(jnp.bfloat16),
                piece_values,
                preferred_element_type=jnp.float32,
            )
            new_rows = summed_rows * jnp.transpose(rescale)[:, :, None] + added_rows
            return (new_max, new_totals, new_rows)

        def keep_state(unused):
            return (row_max, totals, summed_rows)

        return lax.cond(key_start <= jnp.max(block_pos), attend, keep_state, 0)

    row_max, totals, summed_rows = lax.map(
        one_block,
        (start_state[0], start_state[1], start_state[2], query_blocks, pos_blocks, doc_blocks),
    )
    divisor = jnp.transpose(totals, (0, 2, 1))[:, :, :, None]
    attended = (summed_rows / divisor).astype(jnp.bfloat16).reshape(group_rows, heads_here * HDIM)

    def output(block_pair):
        row_block, block_mode = block_pair
        weight = lax.dynamic_index_in_dim(out_weight, block_mode, 0, keepdims=False)
        return jnp.dot(row_block, weight, preferred_element_type=jnp.float32)

    partial_value = lax.map(
        output, (attended.reshape(block_count, BLOCK, attended.shape[1]), block_modes)
    )
    head_sums = lax.psum_scatter(
        partial_value.reshape(group_rows, partial_value.shape[2]).astype(jnp.bfloat16),
        "seq",
        scatter_dimension=0,
        tiled=True,
    ).astype(jnp.float32)
    return (tokens.astype(jnp.float32) + head_sums).astype(jnp.bfloat16)


def solution(mesh):
    return jax.shard_map(
        body,
        mesh=mesh,
        in_specs=(
            P(("mod", "seq"), None),
            P(),
            P(None, None, "seq"),
            P(None, "seq", None),
            P(),
            P(),
        ),
        out_specs=P(("mod", "seq"), None),
        check_vma=False,
    )
```

profile of v0, /device:TPU:0, one launch (start us, length us, event | category | flops | bytes accessed | tf_op | source)
XLA Modules:
  0.0 286.2 jit_solution(8059738032792153300)
XLA Ops:
  6.6 0.8 select_reduce_fusion.2
  7.4 1.2 fusion.48
  8.6 1.3 select_reduce_fusion.1
  9.9 2.0 fusion.50
  12.2 49.6 %all-gather.6.cloned.1.call-done = bf16[512,4096]{1,0:T(8,128)(2,1)} async-done(((bf16[64,4096]{1,0:T(8,128)(2,1)}), bf16[512,4096]{1,0:T(8,128)(2,1)}) %all-gather.6.cloned.1.call-update) | async-done | bytes 4194320 | tf_op jit(solution)/shard_map/all_gather | solution.py:38
  61.7 37.1 %while.33 = (s32[]{:T(128)}, bf16[4,128,1536]{2,1,0:T(8,128)(2,1)S(1)}, bf16[4,128,4096]{2,1,0:T(8,128)(2,1)}, s32[4]{0:T(128)S(1)}, bf16[3,4096,1536]{2,1,0:T(8,128)(2,1)}, /*index=5*/s32[]{:T(128)}, s32[]{:T(128)}, s32[]{:T(128)}) while((s32[]{:T(128)}, bf16[4,128,1536]{2,1,0:T(8,128)(2,1)S(1)}, bf16[4,128,4096]{2,1,0:T(8,128)(2,1)}, ...), condition=%wide.region_4.5_spmd, body=%wide.region_3.4_spmd.sunk | while | flops 1610809344 | bytes 14025863 | solution.py:49
  61.7 0.6 dynamic_slice.95
  64.3 6.7 %fusion.65 = bf16[4,128,1536]{2,1,0:T(8,128)(2,1)S(1)} fusion(bf16[4,128,1536]{2,1,0:T(8,128)(2,1)S(1)} %get-tuple-element.457, s32[]{:T(128)} %get-tuple-element.456, bf16[3,4096,1536]{2,1,0:T(8,128)(2,1)} %get-tuple-element.468, s32[]{:T(128)S(6)} %select_n.67, bf16[4,128,4096]{2,1,0:T(8,128)(2,1)} %get-tuple-element.466), kind=kOutput, calls=%fused_computation.6.clone.1 | convolution fusion | flops 1610809344 | bytes 14025732 | tf_op jit(solution)/shard_map/while/body/eval_jaxpr/dot_general | solution.py:47
  71.0 0.6 dynamic_slice.95
  73.5 6.7 %fusion.65 = bf16[4,128,1536]{2,1,0:T(8,128)(2,1)S(1)} fusion(bf16[4,128,1536]{2,1,0:T(8,128)(2,1)S(1)} %get-tuple-element.457, s32[]{:T(128)} %get-tuple-element.456, bf16[3,4096,1536]{2,1,0:T(8,128)(2,1)} %get-tuple-element.468, s32[]{:T(128)S(6)} %select_n.67, bf16[4,128,4096]{2,1,0:T(8,128)(2,1)} %get-tuple-element.466), kind=kOutput, calls=%fused_computation.6.clone.1 | convolution fusion | flops 1610809344 | bytes 14025732 | tf_op jit(solution)/shard_map/while/body/eval_jaxpr/dot_general | solution.py:47
  80.3 0.6 dynamic_slice.95
  82.8 6.7 %fusion.65 = bf16[4,128,1536]{2,1,0:T(8,128)(2,1)S(1)} fusion(bf16[4,128,1536]{2,1,0:T(8,128)(2,1)S(1)} %get-tuple-element.457, s32[]{:T(128)} %get-tuple-element.456, bf16[3,4096,1536]{2,1,0:T(8,128)(2,1)} %get-tuple-element.468, s32[]{:T(128)S(6)} %select_n.67, bf16[4,128,4096]{2,1,0:T(8,128)(2,1)} %get-tuple-element.466), kind=kOutput, calls=%fused_computation.6.clone.1 | convolution fusion | flops 1610809344 | bytes 14025732 | tf_op jit(solution)/shard_map/while/body/eval_jaxpr/dot_general | solution.py:47
  89.5 0.6 dynamic_slice.95
  92.1 6.7 %fusion.65 = bf16[4,128,1536]{2,1,0:T(8,128)(2,1)S(1)} fusion(bf16[4,128,1536]{2,1,0:T(8,128)(2,1)S(1)} %get-tuple-element.457, s32[]{:T(128)} %get-tuple-element.456, bf16[3,4096,1536]{2,1,0:T(8,128)(2,1)} %get-tuple-element.468, s32[]{:T(128)S(6)} %select_n.67, bf16[4,128,4096]{2,1,0:T(8,128)(2,1)} %get-tuple-element.466), kind=kOutput, calls=%fused_computation.6.clone.1 | convolution fusion | flops 1610809344 | bytes 14025732 | tf_op jit(solution)/shard_map/while/body/eval_jaxpr/dot_general | solution.py:47
  98.8 1.1 copy.14
  99.9 0.6 reshape.161
  100.6 1.1 fusion.53
  101.8 0.7 all-gather.10.cloned.1.call-update
  102.9 0.3 copy.15
  103.3 32.5 %all-gather.8.cloned.1.call-done = bf16[2048,4,1,128]{0,3,2,1:T(8,128)(2,1)} async-done(((bf16[512,4,1,128]{0,3,2,1:T(8,128)(2,1)}), bf16[2048,4,1,128]{0,3,2,1:T(8,128)(2,1)}) %all-gather.8.cloned.1.call-update) | async-done | bytes 2097168 | tf_op jit(solution)/shard_map/all_gather | solution.py:72
  135.7 3.0 %copy.17 = bf16[2048,4,128]{2,0,1:T(8,128)(2,1)S(1)} copy(bf16[2048,4,128]{0,2,1:T(8,128)(2,1)} %bitcast.85) | data formatting | bytes 4194304
  138.8 33.9 %all-gather.10.cloned.1.call-done = bf16[2048,4,1,128]{0,3,2,1:T(8,128)(2,1)} async-done(((bf16[512,4,1,128]{0,3,2,1:T(8,128)(2,1)}), bf16[2048,4,1,128]{0,3,2,1:T(8,128)(2,1)}) %all-gather.10.cloned.1.call-update) | async-done | bytes 2097168 | tf_op jit(solution)/shard_map/all_gather | solution.py:73
  172.7 4.0 %copy.18 = bf16[2048,4,128]{2,0,1:T(8,128)(2,1)} copy(bf16[2048,4,128]{0,2,1:T(8,128)(2,1)} %bitcast.86) | data formatting | bytes 4194304
  176.6 23.8 %while.35 = (s32[]{:T(128)}, f32[4,4,128]{2,1,0:T(4,128)S(1)}, f32[4,128,4,128]{1,3,2,0:T(8,128)}, s32[4,128]{1,0:T(4,128)S(1)}, s32[2048]{0:T(1024)S(1)}, /*ind...) while((s32[]{:T(128)}, f32[4,4,128]{2,1,0:T(4,128)S(1)}, ...), condition=%wide.region_14.15_spmd.clone, body=%wide.region_8.14_spmd.clone.sunk | while | flops 549324416 | bytes 28503860 | solution.py:110
  176.6 0.6 fusion.69
  178.0 3.7 %conditional.3 = (f32[1,4,128]{2,1,0:T(4,128)S(1)}, f32[1,128,4,128]{3,1,2,0:T(8,128)S(1)}) conditional(s32[]{:T(128)} %convert_element_type.82, (f32[4,128]{1,0:T(4,128)S(1)}, f32[128,4,128]{2,0,1:T(8,128)S(1)}) %tuple.105, (s32[2048]{0:T(1024)S(1)}, s32[1,128]{1,0:T(1,128)S(1)}, s32[2048]{0:T(1024)S(1)}, s32[4,128]{1,0:T(4,128)S(1)}, s32[]{:T(128)}, ...), branch_computations={%region_10.10_spmd, %region_11.13_spmd} | conditional | flops 549324288 | bytes 26912820 | solution.py:108
  178.0 0.3 compare_and_fusion
  178.3 1.0 select_reduce_fusion
  179.3 1.2 fusion.18
  180.5 1.2 fusion.31
  181.8 0.7 constant_dynamic-update-slice_fusion.5
  182.5 0.6 fusion.69
  183.9 3.7 %conditional.3 = (f32[1,4,128]{2,1,0:T(4,128)S(1)}, f32[1,128,4,128]{3,1,2,0:T(8,128)S(1)}) conditional(s32[]{:T(128)} %convert_element_type.82, (f32[4,128]{1,0:T(4,128)S(1)}, f32[128,4,128]{2,0,1:T(8,128)S(1)}) %tuple.105, (s32[2048]{0:T(1024)S(1)}, s32[1,128]{1,0:T(1,128)S(1)}, s32[2048]{0:T(1024)S(1)}, s32[4,128]{1,0:T(4,128)S(1)}, s32[]{:T(128)}, ...), branch_computations={%region_10.10_spmd, %region_11.13_spmd} | conditional | flops 549324288 | bytes 26912820 | solution.py:108
  183.9 0.3 compare_and_fusion
  184.2 1.0 select_reduce_fusion
  185.2 1.2 fusion.18
  186.4 1.2 fusion.31
  187.7 0.7 constant_dynamic-update-slice_fusion.5
  188.5 0.6 fusion.69
  189.8 3.7 %conditional.3 = (f32[1,4,128]{2,1,0:T(4,128)S(1)}, f32[1,128,4,128]{3,1,2,0:T(8,128)S(1)}) conditional(s32[]{:T(128)} %convert_element_type.82, (f32[4,128]{1,0:T(4,128)S(1)}, f32[128,4,128]{2,0,1:T(8,128)S(1)}) %tuple.105, (s32[2048]{0:T(1024)S(1)}, s32[1,128]{1,0:T(1,128)S(1)}, s32[2048]{0:T(1024)S(1)}, s32[4,128]{1,0:T(4,128)S(1)}, s32[]{:T(128)}, ...), branch_computations={%region_10.10_spmd, %region_11.13_spmd} | conditional | flops 549324288 | bytes 26912820 | solution.py:108
  189.9 0.3 compare_and_fusion
  190.2 1.0 select_reduce_fusion
  191.2 1.2 fusion.18
  192.3 1.2 fusion.31
  193.7 0.7 constant_dynamic-update-slice_fusion.5
  194.4 0.6 fusion.69
  195.8 3.7 %conditional.3 = (f32[1,4,128]{2,1,0:T(4,128)S(1)}, f32[1,128,4,128]{3,1,2,0:T(8,128)S(1)}) conditional(s32[]{:T(128)} %convert_element_type.82, (f32[4,128]{1,0:T(4,128)S(1)}, f32[128,4,128]{2,0,1:T(8,128)S(1)}) %tuple.105, (s32[2048]{0:T(1024)S(1)}, s32[1,128]{1,0:T(1,128)S(1)}, s32[2048]{0:T(1024)S(1)}, s32[4,128]{1,0:T(4,128)S(1)}, s32[]{:T(128)}, ...), branch_computations={%region_10.10_spmd, %region_11.13_spmd} | conditional | flops 549324288 | bytes 26912820 | solution.py:108
  195.8 0.3 compare_and_fusion
  196.1 1.0 select_reduce_fusion
  197.1 1.2 fusion.18
  198.3 1.2 fusion.31
  199.6 0.7 constant_dynamic-update-slice_fusion.5
  200.4 1.3 divide_convert_fusion
  201.7 25.9 %while.34 = (s32[]{:T(128)}, bf16[4,128,4096]{2,1,0:T(8,128)(2,1)}, bf16[4,128,512]{1,2,0:T(8,128)(2,1)S(1)}, s32[4]{0:T(128)S(1)}, bf16[3,512,4096]{2,1,0:T(8,128)(2,1)}, /*index=5*/s32[]{:T(128)}, s32[]{:T(128)}, s32[]{:T(128)}) while((s32[]{:T(128)}, bf16[4,128,4096]{2,1,0:T(8,128)(2,1)}, bf16[4,128,512]{1,2,0:T(8,128)(2,1)S(1)}, ...), condition=%wide.region_16.17_spmd, body=%wide.region_15.16_spmd.sunk | while | flops 536870912 | bytes 6423687 | solution.py:122
  201.7 0.6 dynamic_slice.98
  204.3 3.9 %fusion.68 = bf16[4,128,4096]{2,1,0:T(8,128)(2,1)} fusion(bf16[4,128,4096]{2,1,0:T(8,128)(2,1)} %get-tuple-element.517, s32[]{:T(128)} %get-tuple-element.516, bf16[3,512,4096]{2,1,0:T(8,128)(2,1)} %get-tuple-element.528, s32[]{:T(128)S(6)} %select_n.68, bf16[4,128,512]{1,2,0:T(8,128)(2,1)S(1)} %get-tuple-element.526), kind=kOutput, calls=%fused_computation.36.clone.1 | convolution fusion | flops 536870912 | bytes 6423556 | tf_op jit(solution)/shard_map/while/body/eval_jaxpr/dot_general | solution.py:120
  208.2 0.6 dynamic_slice.98
  210.7 4.0 %fusion.68 = bf16[4,128,4096]{2,1,0:T(8,128)(2,1)} fusion(bf16[4,128,4096]{2,1,0:T(8,128)(2,1)} %get-tuple-element.517, s32[]{:T(128)} %get-tuple-element.516, bf16[3,512,4096]{2,1,0:T(8,128)(2,1)} %get-tuple-element.528, s32[]{:T(128)S(6)} %select_n.68, bf16[4,128,512]{1,2,0:T(8,128)(2,1)S(1)} %get-tuple-element.526), kind=kOutput, calls=%fused_computation.36.clone.1 | convolution fusion | flops 536870912 | bytes 6423556 | tf_op jit(solution)/shard_map/while/body/eval_jaxpr/dot_general | solution.py:120
  214.7 0.6 dynamic_slice.98
  217.3 3.9 %fusion.68 = bf16[4,128,4096]{2,1,0:T(8,128)(2,1)} fusion(bf16[4,128,4096]{2,1,0:T(8,128)(2,1)} %get-tuple-element.517, s32[]{:T(128)} %get-tuple-element.516, bf16[3,512,4096]{2,1,0:T(8,128)(2,1)} %get-tuple-element.528, s32[]{:T(128)S(6)} %select_n.68, bf16[4,128,512]{1,2,0:T(8,128)(2,1)S(1)} %get-tuple-element.526), kind=kOutput, calls=%fused_computation.36.clone.1 | convolution fusion | flops 536870912 | bytes 6423556 | tf_op jit(solution)/shard_map/while/body/eval_jaxpr/dot_general | solution.py:120
  221.2 0.6 dynamic_slice.98
  223.7 3.9 %fusion.68 = bf16[4,128,4096]{2,1,0:T(8,128)(2,1)} fusion(bf16[4,128,4096]{2,1,0:T(8,128)(2,1)} %get-tuple-element.517, s32[]{:T(128)} %get-tuple-element.516, bf16[3,512,4096]{2,1,0:T(8,128)(2,1)} %get-tuple-element.528, s32[]{:T(128)S(6)} %select_n.68, bf16[4,128,512]{1,2,0:T(8,128)(2,1)S(1)} %get-tuple-element.526), kind=kOutput, calls=%fused_computation.36.clone.1 | convolution fusion | flops 536870912 | bytes 6423556 | tf_op jit(solution)/shard_map/while/body/eval_jaxpr/dot_general | solution.py:120
  227.7 50.1 %reduce-scatter.2.cloned.1.call-done = bf16[64,4096]{1,0:T(8,128)(2,1)} async-done(((bf16[512,4096]{1,0:T(8,128)(2,1)}), bf16[64,4096]{1,0:T(8,128)(2,1)}) %reduce-scatter.2.cloned.1.call-update) | async-done | bytes 524304 | tf_op jit(solution)/shard_map/reduce_scatter | solution.py:125
  277.8 2.0 fusion.51
  (75 shorter events, 1.6 us)
Async XLA Ops:
  6.5 5.5 %copy-start.2 = (s32[16]{0:T(128)S(1)}, s32[16]{0:T(128)}, u32[]{:S(2)}) copy-start(s32[16]{0:T(128)} %param.18) | copy-start | bytes 196
  6.5 55.2 %all-gather.6.cloned.1.call-start = ((), (), s32[]{:S(2)}) async-start(), calls=%async_computation.1 | async-start | bytes 4718592 | tf_op jit(solution)/shard_map/all_gather | solution.py:38
  12.0 123.8 %all-gather.8.cloned.1.call-start = ((), (), s32[]{:S(2)}) async-start(), calls=%async_computation.3 | async-start | bytes 2621440 | tf_op jit(solution)/shard_map/all_gather | solution.py:72
  99.9 2.6 copy-start.3
  101.7 70.9 %all-gather.10.cloned.1.call-start = ((), (), s32[]{:S(2)}) async-start(), calls=%async_computation.4 | async-start | bytes 2621440 | tf_op jit(solution)/shard_map/all_gather | solution.py:73
  102.5 175.3 %reduce-scatter.2.cloned.1.call-start = ((), (), s32[]{:S(2)}) async-start(), calls=%async_computation.2 | async-start | bytes 4718592 | tf_op jit(solution)/shard_map/reduce_scatter | solution.py:125
  178.3 2.2 copy-start.1
  184.2 2.2 copy-start.1
  190.2 2.2 copy-start.1
  196.1 2.2 copy-start.1
  227.6 50.1 %copy-start = (bf16[64,4096]{1,0:T(8,128)(2,1)S(1)}, bf16[64,4096]{1,0:T(8,128)(2,1)}, u32[]{:S(2)}) copy-start(bf16[64,4096]{1,0:T(8,128)(2,1)} %param.14) | copy-start | bytes 1572868
Sparse Core Ops, SparseCore 0:
  12.1 49.5 all-gather.5
  101.9 33.8 all-gather.7
  137.6 35.0 all-gather.9
  227.8 49.9 reduce-scatter.1
where the time goes:
time: 287 us; the launch traced here: 286 us
  waiting for transfers between devices  167 us (58%)
  matrix products  51.3 us (18%)
  local copies, waits for them, and re-layouts  18.7 us (7%)
  loops' own time  18.6 us (6%)
  other arithmetic  17.4 us (6%)
  between operations  13.3 us (5%)
    reduce_scatter x1, waiting for transfers between devices, body(): lax.psum_scatter(partial_value.reshape(group_rows, partial_value.shape[2]...  50.1 us
    all_gather x1, waiting for transfers between devices, body(): gathered = lax.all_gather(normed, 'seq', axis=0, tiled=True)  49.6 us
    all_gather x1, waiting for transfers between devices, body(): piece_values = lax.all_gather(values_here, 'mod', axis=0, tiled=True)  33.9 us
    all_gather x1, waiting for transfers between devices, body(): piece_keys = lax.all_gather(keys_here, 'mod', axis=0, tiled=True)  32.5 us
    dot_general x4, matrix products, project(): jnp.dot(row_block, weight, preferred_element_type=jnp.float32)  26.9 us
    dot_general x4, matrix products, output(): return jnp.dot(row_block, weight, preferred_element_type=jnp.float32)  15.8 us
    another operation x1, loops' own time, body(): lax.map(project, (gathered.reshape(block_count, BLOCK, gathered.shape[1])...  7.85 us
    another operation x1, loops' own time, body(): lax.map(output, (attended.reshape(block_count, BLOCK, attended.shape[1]),...  7.79 us
  transfers between devices with their start and end apart: 4, of which 4 were waited for; matrix products, arithmetic and copies ran while one was open for 1% of the time, Pallas kernels for 0%

commit v1 on v0

--- a/solution.py
+++ b/solution.py
@@ -69,8 +69,13 @@
         jnp.zeros((block_total, block_size, heads_here, HDIM), jnp.float32),
     )
     key_start = jnp.int32(0)
-    piece_keys = lax.all_gather(keys_here, "mod", axis=0, tiled=True)
-    piece_values = lax.all_gather(values_here, "mod", axis=0, tiled=True)
+    piece_keys, piece_values = jnp.split(
+        lax.all_gather(
+            jnp.concatenate([keys_here, values_here], axis=1), "mod", axis=0, tiled=True
+        ),
+        [keys_here.shape[1]],
+        axis=1,
+    )
     key_count = piece_keys.shape[0]
     key_pos = jnp.arange(key_count, dtype=jnp.int32)
     key_docs = documents(key_pos, doc_lengths)

time: 287 us -> 275 us (0.958)
  waiting for transfers between devices: 167 us -> 150 us
  local copies, waits for them, and re-layouts: 18.7 us -> 22.5 us
    all_gather x2 -> x1, waiting for transfers between devices: 66.4 us -> 50.6 us  [body(): lax.all_gather(jnp.concatenate([keys_here, values_here], axis=1), 'mod',...]
    split x0 -> x1, local copies, waits for them, and re-layouts: none -> 4.78 us  [body(): jnp.split(lax.all_gather(jnp.concatenate([keys_here, values_here], axis=1...]
  transfers between devices with their start and end apart: 4 -> 3, of which waited for: 4 -> 3; matrix products, arithmetic and copies ran while one was open for 1% -> 0% of each run, Pallas kernels for 0% -> 0%
where the time goes in v1:
time: 275 us; the launch traced here: 274 us
  waiting for transfers between devices  150 us (55%)
  matrix products  51.3 us (19%)
  local copies, waits for them, and re-layouts  22.5 us (8%)
  other arithmetic  18.6 us (7%)
  loops' own time  18 us (7%)
  between operations  13.3 us (5%)
    all_gather x1, waiting for transfers between devices, body(): lax.all_gather(jnp.concatenate([keys_here, values_here], axis=1), 'mod',...  50.6 us
    reduce_scatter x1, waiting for transfers between devices, body(): lax.psum_scatter(partial_value.reshape(group_rows, partial_value.shape[2]...  50.1 us
    all_gather x1, waiting for transfers between devices, body(): gathered = lax.all_gather(normed, 'seq', axis=0, tiled=True)  49.6 us
    dot_general x4, matrix products, project(): jnp.dot(row_block, weight, preferred_element_type=jnp.float32)  26.9 us
    dot_general x4, matrix products, output(): return jnp.dot(row_block, weight, preferred_element_type=jnp.float32)  15.8 us
    another operation x1, loops' own time, body(): lax.map(project, (gathered.reshape(block_count, BLOCK, gathered.shape[1])...  7.85 us
    another operation x1, loops' own time, body(): lax.map(output, (attended.reshape(block_count, BLOCK, attended.shape[1]),...  7.44 us
    unnamed x9, local copies, waits for them, and re-layouts  7.06 us
  transfers between devices with their start and end apart: 3, of which 3 were waited for; matrix products, arithmetic and copies ran while one was open for 0% of the time, Pallas kernels for 0%

profile of v1, /device:TPU:0, one launch (start us, length us, event | category | flops | bytes accessed | tf_op | source)
XLA Modules:
  0.0 274.1 jit_solution(4672608113789526536)
XLA Ops:
  6.6 0.8 select_reduce_fusion.2
  7.4 1.2 fusion.48
  8.6 1.3 select_reduce_fusion.1
  9.9 2.0 fusion.50
  12.2 49.6 %all-gather.3.cloned.1.call-done = bf16[512,4096]{1,0:T(8,128)(2,1)} async-done(((bf16[64,4096]{1,0:T(8,128)(2,1)}), bf16[512,4096]{1,0:T(8,128)(2,1)}) %all-gather.3.cloned.1.call-update) | async-done | bytes 4194320 | tf_op jit(solution)/shard_map/all_gather | solution.py:38
  61.7 37.1 %while.33 = (s32[]{:T(128)}, bf16[4,128,1536]{2,1,0:T(8,128)(2,1)S(1)}, bf16[4,128,4096]{2,1,0:T(8,128)(2,1)}, s32[4]{0:T(128)S(1)}, bf16[3,4096,1536]{2,1,0:T(8,128)(2,1)}, /*index=5*/s32[]{:T(128)}, s32[]{:T(128)}, s32[]{:T(128)}) while((s32[]{:T(128)}, bf16[4,128,1536]{2,1,0:T(8,128)(2,1)S(1)}, bf16[4,128,4096]{2,1,0:T(8,128)(2,1)}, ...), condition=%wide.region_4.5_spmd, body=%wide.region_3.4_spmd.sunk | while | flops 1610809344 | bytes 14025863 | solution.py:49
  61.7 0.6 dynamic_slice.95
  64.3 6.7 %fusion.65 = bf16[4,128,1536]{2,1,0:T(8,128)(2,1)S(1)} fusion(bf16[4,128,1536]{2,1,0:T(8,128)(2,1)S(1)} %get-tuple-element.459, s32[]{:T(128)} %get-tuple-element.458, bf16[3,4096,1536]{2,1,0:T(8,128)(2,1)} %get-tuple-element.470, s32[]{:T(128)S(6)} %select_n.67, bf16[4,128,4096]{2,1,0:T(8,128)(2,1)} %get-tuple-element.468), kind=kOutput, calls=%fused_computation.6.clone.1 | convolution fusion | flops 1610809344 | bytes 14025732 | tf_op jit(solution)/shard_map/while/body/eval_jaxpr/dot_general | solution.py:47
  71.0 0.6 dynamic_slice.95
  73.5 6.7 %fusion.65 = bf16[4,128,1536]{2,1,0:T(8,128)(2,1)S(1)} fusion(bf16[4,128,1536]{2,1,0:T(8,128)(2,1)S(1)} %get-tuple-element.459, s32[]{:T(128)} %get-tuple-element.458, bf16[3,4096,1536]{2,1,0:T(8,128)(2,1)} %get-tuple-element.470, s32[]{:T(128)S(6)} %select_n.67, bf16[4,128,4096]{2,1,0:T(8,128)(2,1)} %get-tuple-element.468), kind=kOutput, calls=%fused_computation.6.clone.1 | convolution fusion | flops 1610809344 | bytes 14025732 | tf_op jit(solution)/shard_map/while/body/eval_jaxpr/dot_general | solution.py:47
  80.3 0.6 dynamic_slice.95
  82.8 6.7 %fusion.65 = bf16[4,128,1536]{2,1,0:T(8,128)(2,1)S(1)} fusion(bf16[4,128,1536]{2,1,0:T(8,128)(2,1)S(1)} %get-tuple-element.459, s32[]{:T(128)} %get-tuple-element.458, bf16[3,4096,1536]{2,1,0:T(8,128)(2,1)} %get-tuple-element.470, s32[]{:T(128)S(6)} %select_n.67, bf16[4,128,4096]{2,1,0:T(8,128)(2,1)} %get-tuple-element.468), kind=kOutput, calls=%fused_computation.6.clone.1 | convolution fusion | flops 1610809344 | bytes 14025732 | tf_op jit(solution)/shard_map/while/body/eval_jaxpr/dot_general | solution.py:47
  89.5 0.6 dynamic_slice.95
  92.1 6.7 %fusion.65 = bf16[4,128,1536]{2,1,0:T(8,128)(2,1)S(1)} fusion(bf16[4,128,1536]{2,1,0:T(8,128)(2,1)S(1)} %get-tuple-element.459, s32[]{:T(128)} %get-tuple-element.458, bf16[3,4096,1536]{2,1,0:T(8,128)(2,1)} %get-tuple-element.470, s32[]{:T(128)S(6)} %select_n.67, bf16[4,128,4096]{2,1,0:T(8,128)(2,1)} %get-tuple-element.468), kind=kOutput, calls=%fused_computation.6.clone.1 | convolution fusion | flops 1610809344 | bytes 14025732 | tf_op jit(solution)/shard_map/while/body/eval_jaxpr/dot_general | solution.py:47
  98.8 1.1 copy.15
  99.9 0.6 reshape.161
  100.7 1.2 pad_maximum_fusion
  102.0 0.2 reduce-window.8
  102.4 0.3 copy.16
  102.7 50.6 %all-gather.5.cloned.1.call-done = bf16[2048,8,128]{0,2,1:T(8,128)(2,1)} async-done(((bf16[512,8,128]{0,2,1:T(8,128)(2,1)}), bf16[2048,8,128]{0,2,1:T(8,128)(2,1)}) %all-gather.5.cloned.1.call-update) | async-done | bytes 4194320 | tf_op jit(solution)/shard_map/all_gather | solution.py:73
  153.3 4.8 %fusion.53 = (bf16[2048,4,128]{0,2,1:T(8,128)(2,1)}, bf16[2048,4,128]{0,2,1:T(8,128)(2,1)}) fusion(bf16[2048,8,128]{0,2,1:T(8,128)(2,1)} %all-gather.5.cloned.1.call-done), kind=kLoop, calls=%fused_computation.71 | loop fusion | bytes 8388608 | tf_op jit(solution)/shard_map/split | solution.py:72
  158.1 3.0 %copy.19 = bf16[2048,4,128]{2,0,1:T(8,128)(2,1)S(1)} copy(bf16[2048,4,128]{0,2,1:T(8,128)(2,1)} %get-tuple-element.317) | data formatting | bytes 4194304
  161.1 4.0 %copy.20 = bf16[2048,4,128]{2,0,1:T(8,128)(2,1)} copy(bf16[2048,4,128]{0,2,1:T(8,128)(2,1)} %get-tuple-element.316) | data formatting | bytes 4194304
  165.1 23.5 %while.35 = (s32[]{:T(128)}, f32[4,4,128]{2,1,0:T(4,128)S(1)}, f32[4,128,4,128]{1,3,2,0:T(8,128)}, s32[4,128]{1,0:T(4,128)S(1)}, s32[2048]{0:T(1024)S(1)}, /*ind...) while((s32[]{:T(128)}, f32[4,4,128]{2,1,0:T(4,128)S(1)}, ...), condition=%wide.region_14.15_spmd.clone, body=%wide.region_8.14_spmd.clone.sunk | while | flops 549324416 | bytes 28503860 | solution.py:115
  165.1 0.6 fusion.69
  166.4 3.7 %conditional.3 = (f32[1,4,128]{2,1,0:T(4,128)S(1)}, f32[1,128,4,128]{3,1,2,0:T(8,128)S(1)}) conditional(s32[]{:T(128)} %convert_element_type.82, (f32[4,128]{1,0:T(4,128)S(1)}, f32[128,4,128]{2,0,1:T(8,128)S(1)}) %tuple.106, (s32[2048]{0:T(1024)S(1)}, s32[1,128]{1,0:T(1,128)S(1)}, s32[2048]{0:T(1024)S(1)}, s32[4,128]{1,0:T(4,128)S(1)}, s32[]{:T(128)}, ...), branch_computations={%region_10.10_spmd, %region_11.13_spmd} | conditional | flops 549324288 | bytes 26912820 | solution.py:113
  166.4 0.3 compare_and_fusion
  166.7 1.0 select_reduce_fusion
  167.7 1.2 fusion.18
  168.9 1.2 fusion.31
  170.2 0.7 constant_dynamic-update-slice_fusion.5
  170.9 0.6 fusion.69
  172.2 3.7 %conditional.3 = (f32[1,4,128]{2,1,0:T(4,128)S(1)}, f32[1,128,4,128]{3,1,2,0:T(8,128)S(1)}) conditional(s32[]{:T(128)} %convert_element_type.82, (f32[4,128]{1,0:T(4,128)S(1)}, f32[128,4,128]{2,0,1:T(8,128)S(1)}) %tuple.106, (s32[2048]{0:T(1024)S(1)}, s32[1,128]{1,0:T(1,128)S(1)}, s32[2048]{0:T(1024)S(1)}, s32[4,128]{1,0:T(4,128)S(1)}, s32[]{:T(128)}, ...), branch_computations={%region_10.10_spmd, %region_11.13_spmd} | conditional | flops 549324288 | bytes 26912820 | solution.py:113
  172.3 0.3 compare_and_fusion
  172.6 1.0 select_reduce_fusion
  173.6 1.2 fusion.18
  174.7 1.2 fusion.31
  176.1 0.7 constant_dynamic-update-slice_fusion.5
  176.8 0.6 fusion.69
  178.1 3.7 %conditional.3 = (f32[1,4,128]{2,1,0:T(4,128)S(1)}, f32[1,128,4,128]{3,1,2,0:T(8,128)S(1)}) conditional(s32[]{:T(128)} %convert_element_type.82, (f32[4,128]{1,0:T(4,128)S(1)}, f32[128,4,128]{2,0,1:T(8,128)S(1)}) %tuple.106, (s32[2048]{0:T(1024)S(1)}, s32[1,128]{1,0:T(1,128)S(1)}, s32[2048]{0:T(1024)S(1)}, s32[4,128]{1,0:T(4,128)S(1)}, s32[]{:T(128)}, ...), branch_computations={%region_10.10_spmd, %region_11.13_spmd} | conditional | flops 549324288 | bytes 26912820 | solution.py:113
  178.1 0.3 compare_and_fusion
  178.4 1.0 select_reduce_fusion
  179.4 1.2 fusion.18
  180.6 1.2 fusion.31
  181.9 0.7 constant_dynamic-update-slice_fusion.5
  182.7 0.6 fusion.69
  184.0 3.7 %conditional.3 = (f32[1,4,128]{2,1,0:T(4,128)S(1)}, f32[1,128,4,128]{3,1,2,0:T(8,128)S(1)}) conditional(s32[]{:T(128)} %convert_element_type.82, (f32[4,128]{1,0:T(4,128)S(1)}, f32[128,4,128]{2,0,1:T(8,128)S(1)}) %tuple.106, (s32[2048]{0:T(1024)S(1)}, s32[1,128]{1,0:T(1,128)S(1)}, s32[2048]{0:T(1024)S(1)}, s32[4,128]{1,0:T(4,128)S(1)}, s32[]{:T(128)}, ...), branch_computations={%region_10.10_spmd, %region_11.13_spmd} | conditional | flops 549324288 | bytes 26912820 | solution.py:113
  184.0 0.3 compare_and_fusion
  184.3 1.0 select_reduce_fusion
  185.3 1.2 fusion.18
  186.5 1.2 fusion.31
  187.8 0.7 constant_dynamic-update-slice_fusion.5
  188.6 1.3 divide_convert_fusion
  189.9 25.6 %while.34 = (s32[]{:T(128)}, bf16[4,128,4096]{2,1,0:T(8,128)(2,1)}, bf16[4,128,512]{1,2,0:T(8,128)(2,1)S(1)}, s32[4]{0:T(128)S(1)}, bf16[3,512,4096]{2,1,0:T(8,128)(2,1)}, /*index=5*/s32[]{:T(128)}, s32[]{:T(128)}, s32[]{:T(128)}) while((s32[]{:T(128)}, bf16[4,128,4096]{2,1,0:T(8,128)(2,1)}, bf16[4,128,512]{1,2,0:T(8,128)(2,1)S(1)}, ...), condition=%wide.region_16.17_spmd, body=%wide.region_15.16_spmd.sunk | while | flops 536870912 | bytes 6423687 | solution.py:127
  189.9 0.6 dynamic_slice.98
  192.4 3.9 %fusion.68 = bf16[4,128,4096]{2,1,0:T(8,128)(2,1)} fusion(bf16[4,128,4096]{2,1,0:T(8,128)(2,1)} %get-tuple-element.519, s32[]{:T(128)} %get-tuple-element.518, bf16[3,512,4096]{2,1,0:T(8,128)(2,1)} %get-tuple-element.530, s32[]{:T(128)S(6)} %select_n.68, bf16[4,128,512]{1,2,0:T(8,128)(2,1)S(1)} %get-tuple-element.528), kind=kOutput, calls=%fused_computation.36.clone.1 | convolution fusion | flops 536870912 | bytes 6423556 | tf_op jit(solution)/shard_map/while/body/eval_jaxpr/dot_general | solution.py:125
  196.3 0.6 dynamic_slice.98
  198.8 4.0 %fusion.68 = bf16[4,128,4096]{2,1,0:T(8,128)(2,1)} fusion(bf16[4,128,4096]{2,1,0:T(8,128)(2,1)} %get-tuple-element.519, s32[]{:T(128)} %get-tuple-element.518, bf16[3,512,4096]{2,1,0:T(8,128)(2,1)} %get-tuple-element.530, s32[]{:T(128)S(6)} %select_n.68, bf16[4,128,512]{1,2,0:T(8,128)(2,1)S(1)} %get-tuple-element.528), kind=kOutput, calls=%fused_computation.36.clone.1 | convolution fusion | flops 536870912 | bytes 6423556 | tf_op jit(solution)/shard_map/while/body/eval_jaxpr/dot_general | solution.py:125
  202.7 0.6 dynamic_slice.98
  205.2 3.9 %fusion.68 = bf16[4,128,4096]{2,1,0:T(8,128)(2,1)} fusion(bf16[4,128,4096]{2,1,0:T(8,128)(2,1)} %get-tuple-element.519, s32[]{:T(128)} %get-tuple-element.518, bf16[3,512,4096]{2,1,0:T(8,128)(2,1)} %get-tuple-element.530, s32[]{:T(128)S(6)} %select_n.68, bf16[4,128,512]{1,2,0:T(8,128)(2,1)S(1)} %get-tuple-element.528), kind=kOutput, calls=%fused_computation.36.clone.1 | convolution fusion | flops 536870912 | bytes 6423556 | tf_op jit(solution)/shard_map/while/body/eval_jaxpr/dot_general | solution.py:125
  209.1 0.6 dynamic_slice.98
  211.6 3.9 %fusion.68 = bf16[4,128,4096]{2,1,0:T(8,128)(2,1)} fusion(bf16[4,128,4096]{2,1,0:T(8,128)(2,1)} %get-tuple-element.519, s32[]{:T(128)} %get-tuple-element.518, bf16[3,512,4096]{2,1,0:T(8,128)(2,1)} %get-tuple-element.530, s32[]{:T(128)S(6)} %select_n.68, bf16[4,128,512]{1,2,0:T(8,128)(2,1)S(1)} %get-tuple-element.528), kind=kOutput, calls=%fused_computation.36.clone.1 | convolution fusion | flops 536870912 | bytes 6423556 | tf_op jit(solution)/shard_map/while/body/eval_jaxpr/dot_general | solution.py:125
  215.5 50.1 %reduce-scatter.2.cloned.1.call-done = bf16[64,4096]{1,0:T(8,128)(2,1)} async-done(((bf16[512,4096]{1,0:T(8,128)(2,1)}), bf16[64,4096]{1,0:T(8,128)(2,1)}) %reduce-scatter.2.cloned.1.call-update) | async-done | bytes 524304 | tf_op jit(solution)/shard_map/reduce_scatter | solution.py:130
  265.6 2.0 fusion.51
  (74 shorter events, 1.4 us)
Async XLA Ops:
  6.5 5.5 %copy-start.2 = (s32[16]{0:T(128)S(1)}, s32[16]{0:T(128)}, u32[]{:S(2)}) copy-start(s32[16]{0:T(128)} %param.18) | copy-start | bytes 196
  6.5 55.2 %all-gather.3.cloned.1.call-start = ((), (), s32[]{:S(2)}) async-start(), calls=%async_computation.1 | async-start | bytes 4718592 | tf_op jit(solution)/shard_map/all_gather | solution.py:38
  12.0 141.3 %all-gather.5.cloned.1.call-start = ((), (), s32[]{:S(2)}) async-start(), calls=%async_computation.2 | async-start | bytes 5242880 | tf_op jit(solution)/shard_map/all_gather | solution.py:73
  99.9 2.0 copy-start.3
  101.9 163.7 %reduce-scatter.2.cloned.1.call-start = ((), (), s32[]{:S(2)}) async-start(), calls=%async_computation.3 | async-start | bytes 4718592 | tf_op jit(solution)/shard_map/reduce_scatter | solution.py:130
  166.7 2.2 copy-start.1
  172.6 2.2 copy-start.1
  178.4 2.2 copy-start.1
  184.3 2.2 copy-start.1
  215.5 50.1 %copy-start = (bf16[64,4096]{1,0:T(8,128)(2,1)S(1)}, bf16[64,4096]{1,0:T(8,128)(2,1)}, u32[]{:S(2)}) copy-start(bf16[64,4096]{1,0:T(8,128)(2,1)} %param.14) | copy-start | bytes 1572868
Sparse Core Ops, SparseCore 0:
  12.1 49.5 all-gather.2
  102.0 51.2 all-gather.4
  215.6 49.9 reduce-scatter.1
